TPU v7x, 32 devices: a whole 2x2x4 slice. The times are simulated.
32 devices in a mesh: sp: 16 (over z, x, core), dp: 2 (over y).
Axes of the slice: x: 2, y: 2, z: 4, core: 2. Of those that a mesh axis runs over, the one named last changes fastest.
Arguments:
- queries: bfloat16 [1536, 24, 128], P(('dp', 'sp')), parts along dimension 0, may hold values from -12 to 12
- keys: bfloat16 [1536, 24, 128], P(('dp', 'sp')), parts along dimension 0, may hold values from -6 to 6
- values: bfloat16 [1536, 24, 128], P(('dp', 'sp')), parts along dimension 0, may hold values from -6 to 6
Outputs:
- attended: bfloat16 [1536, 3072], P(('dp', 'sp')), parts along dimension 0
There are 2 independent parts, one for each index of `dp`. A program takes and returns all parts, laid end to end along the dimension named above; each array names one. Nothing has to cross between parts.
All inputs are finite; a program needn't handle non-finite values.
Results may differ from a plain program's by a relative error of at most 0.0049.
Values may be sent and summed in bfloat16 or wider, within the bound.
A program may use at most 64 MiB of HBM per device.

v0:
```python
import functools
import math

import jax
import jax.numpy as jnp
from jax import lax
from jax.experimental import pallas as pl
from jax.experimental.pallas import tpu as pltpu
from jax.sharding import PartitionSpec as P

HGROUPS = 8
MESH = pl.DeviceIdType.MESH


def order_of(group, groups):
    half = groups // 2
    side = group // half
    far = [(1 - side) * half + lax.rem(group + step, half) for step in range(half)]
    near = [side * half + lax.rem(group + step, half) for step in range(1, half)]
    return far, near


def ranked(group, groups):
    half = groups // 2
    side, place = group // half, lax.rem(group, half)
    far = [(1 - side) * half + step for step in range(half)]
    near = [side * half + step + (step + half - place) // half for step in range(half - 1)]
    return far, near


def kernel(
    groups, blocks, per_group,
    q_hbm, k_hbm, v_hbm, landed,
    raw, wide, send, held, result,
    in_sem, send_sem, recv_sem, pass_sem, took_sem, back_sem, home_sem,
):
    me = lax.axis_index("sp")
    group, block = me // blocks, lax.rem(me, blocks)
    tokens, heads, width = q_hbm.shape
    half = groups // 2
    side = group // half
    far, near = order_of(group, groups)
    partners = [lax.rem(block + step, blocks) for step in range(1, blocks)]

    loads = [
        pltpu.make_async_copy(src, raw.at[i], in_sem.at[i])
        for i, src in enumerate((q_hbm, k_hbm, v_hbm))
    ]
    for load in loads:
        load.start()

    barrier = pltpu.get_barrier_semaphore()
    for other in far + near:
        pl.semaphore_signal(barrier, inc=1, device_id={"sp": other * blocks + block}, device_id_type=MESH)
    for partner in partners:
        pl.semaphore_signal(barrier, inc=1, device_id={"sp": group * blocks + partner}, device_id_type=MESH)

    for i, load in enumerate(loads):
        load.wait()
        wide[i] = raw[i].astype(jnp.float32).reshape(tokens * heads, width)

    def outward(j, other, part):
        return pltpu.make_async_remote_copy(
            src_ref=send.at[other, j],
            dst_ref=held.at[j, block, group],
            send_sem=send_sem,
            recv_sem=recv_sem.at[j, part],
            device_id={"sp": other * blocks + block},
            device_id_type=MESH,
        )

    def own(j):
        return pltpu.make_async_copy(send.at[group, j], held.at[j, block, group], recv_sem.at[j, 0])

    def sources(part):
        return pl.ds((side if part == 0 else 1 - side) * half, half)

    def arrived(j, part):
        whole = held.at[j, block, sources(part)]
        pltpu.make_async_copy(whole, whole, recv_sem.at[j, part]).wait()

    def share(j, part, partner):
        piece = held.at[j, block, sources(part), pl.ds(1, 2)]
        return pltpu.make_async_remote_copy(
            src_ref=piece,
            dst_ref=piece,
            send_sem=pass_sem.at[partner],
            recv_sem=took_sem.at[j, block],
            device_id={"sp": group * blocks + partner},
            device_id_type=MESH,
        )

    def shared(j, partner):
        whole = held.at[j, partner, :, pl.ds(1, 2)]
        pltpu.make_async_copy(whole, whole, took_sem.at[j, partner]).wait()

    def columns(of, j):
        return pl.ds(pl.multiple_of((of * per_group + j) * width, width), width)

    def back(j, other):
        return pltpu.make_async_remote_copy(
            src_ref=result.at[j, other],
            dst_ref=landed.at[:, columns(group, j)],
            send_sem=back_sem,
            recv_sem=home_sem,
            device_id={"sp": other * blocks + block},
            device_id_type=MESH,
        )

    def own_back(j):
        return pltpu.make_async_copy(result.at[j, group], landed.at[:, columns(group, j)], home_sem)

    for j in range(per_group):
        for to in range(groups):
            head = to * per_group + j
            for i in range(3):
                rows = wide[i, pl.ds(head, tokens, stride=heads), :]
                send[to, j, i] = rows.astype(jnp.bfloat16)
        if j == 0:
            pl.semaphore_wait(barrier, groups - 1 + blocks - 1)
        for other in far:
            outward(j, other, 1).start()
        for other in near:
            outward(j, other, 0).start()
        own(j).start()

    factor = math.log2(math.e) / math.sqrt(width)
    far, near = ranked(group, groups)
    for j in range(per_group):
        for part in range(2):
            arrived(j, part)
            for partner in partners:
                share(j, part, partner).start()
        for partner in partners:
            shared(j, partner)
        keys = held[j, :, :, 1].reshape(-1, width)
        values = held[j, :, :, 2].reshape(-1, width)
        if j == per_group - 1:
            @pl.when(side == 0)
            def release():
                for earlier in (1,):
                    for other in far:
                        back(earlier, other).start()

        for first, picked in (((1 - side) * half, far), (side * half, near)):
            queries = held[j, block, pl.ds(first, half), 0].reshape(half * tokens, width)
            scores = lax.dot_general(
                queries, keys, (((1,), (1,)), ((), ())), preferred_element_type=jnp.float32
            )
            top = jnp.max(scores, axis=-1, keepdims=True)
            weights = jnp.exp2((scores - top) * factor)
            total = jnp.sum(weights, axis=-1, keepdims=True)
            attended = jnp.dot(
                weights.astype(jnp.bfloat16), values, preferred_element_type=jnp.float32
            ) / total
            result[j, pl.ds(first, half)] = attended.astype(jnp.bfloat16).reshape(half, tokens, width)
            if picked is far and j in (1,):
                @pl.when(side > 0)
                def forward():
                    for other in picked:
                        back(j, other).start()
            else:
                for other in picked:
                    back(j, other).start()
        own_back(j).start()

    sent = send.at[pl.ds(0, groups - 1)]
    pltpu.make_async_copy(sent, sent, send_sem).wait()
    for partner in partners:
        passed = held.at[:, block, :, pl.ds(1, 2)]
        pltpu.make_async_copy(passed, passed, pass_sem.at[partner]).wait()
    given = result.at[:, pl.ds(0, groups - 1)]
    pltpu.make_async_copy(given, given, back_sem).wait()
    pltpu.make_async_copy(landed, landed, home_sem).wait()


def shards(queries, keys, values):
    tokens, heads, width = queries.shape
    groups = HGROUPS
    blocks = lax.axis_size("sp") // groups
    per_group = heads // groups
    kind = queries.dtype
    return pl.pallas_call(
        functools.partial(kernel, groups, blocks, per_group),
        out_shape=pltpu.VMEM((tokens, heads * width), kind),
        in_specs=[pl.BlockSpec(memory_space=pl.ANY)] * 3,
        out_specs=pl.BlockSpec(memory_space=pltpu.VMEM),
        scratch_shapes=[
            pltpu.VMEM((3, tokens, heads, width), kind),
            pltpu.VMEM((3, tokens * heads, width), jnp.float32),
            pltpu.VMEM((groups, per_group, 3, tokens, width), kind),
            pltpu.VMEM((per_group, blocks, groups, 3, tokens, width), kind),
            pltpu.VMEM((per_group, groups, tokens, width), kind),
            pltpu.SemaphoreType.DMA((3,)),
            pltpu.SemaphoreType.DMA,
            pltpu.SemaphoreType.DMA((per_group, 2)),
            pltpu.SemaphoreType.DMA((blocks,)),
            pltpu.SemaphoreType.DMA((per_group, blocks)),
            pltpu.SemaphoreType.DMA,
            pltpu.SemaphoreType.DMA,
        ],
        compiler_params=pltpu.CompilerParams(collective_id=0, has_side_effects=True),
    )(queries, keys, values)


def solution(mesh):
    return jax.shard_map(
        shards,
        mesh=mesh,
        in_specs=(
            P(("dp", "sp"), None, None),
            P(("dp", "sp"), None, None),
            P(("dp", "sp"), None, None),
        ),
        out_specs=P(("dp", "sp"), None),
        check_vma=False,
    )
```

profile of v0, /device:TPU:0, one launch (start us, length us, event | category | flops | bytes accessed | tf_op | source)
XLA Modules:
  0.0 34.3 jit_solution(13147880560011908619)
XLA Ops:
  0.0 33.5 %shard_map.37 = bf16[48,3072]{1,0:T(8,128)(2,1)S(1)} custom-call(bf16[48,24,128]{2,1,0:T(8,128)(2,1)} %q_hbm.1, bf16[48,24,128]{2,1,0:T(8,128)(2,1)} %k_hbm.1, bf16[48,24,128]{2,1,0:T(8,128)(2,1)} %v_hbm.1), custom_call_target="tpu_custom_call" | custom-call | tf_op jit(solution)/shard_map/pallas_call | solution.py:183
  33.6 0.7 %copy.5 = bf16[48,3072]{1,0:T(8,128)(2,1)} copy(bf16[48,3072]{1,0:T(8,128)(2,1)S(1)} %shard_map.37) | data formatting | bytes 589824
where the time goes:
time: 34.4 us; the launch traced here: 34.3 us
  Pallas kernels  33.5 us (97%)
  local copies, waits for them, and re-layouts  0.72 us (2%)
    pallas_call x1, Pallas kernels, shards(): pl.pallas_call(functools.partial(kernel, groups, blocks, per_group), out_...  33.5 us
    unnamed x1, local copies, waits for them, and re-layouts  0.72 us

commit v1 on v0

--- a/solution.py
+++ b/solution.py
@@ -9,6 +9,7 @@
 from jax.sharding import PartitionSpec as P
 
 HGROUPS = 8
+COLUMNS = 2
 MESH = pl.DeviceIdType.MESH
 
 
@@ -32,7 +33,7 @@
     groups, blocks, per_group,
     q_hbm, k_hbm, v_hbm, landed,
     raw, wide, send, held, result,
-    in_sem, send_sem, recv_sem, pass_sem, took_sem, back_sem, home_sem,
+    in_sem, send_sem, recv_sem, pass_sem, took_sem, back_sem, home_sem, known,
 ):
     me = lax.axis_index("sp")
     group, block = me // blocks, lax.rem(me, blocks)
@@ -49,9 +50,28 @@
     for load in loads:
         load.start()
 
+    rows = groups // COLUMNS
+    row, column = group // COLUMNS, lax.rem(group, COLUMNS)
+    above, below = row < rows - 1, row > 0
+    across = row * COLUMNS + 1 - column
+
+    def at(step, other_column):
+        return (row + step) * COLUMNS + other_column
+
+    def greet(semaphore, other):
+        pl.semaphore_signal(semaphore, inc=1, device_id={"sp": other * blocks + block}, device_id_type=MESH)
+
     barrier = pltpu.get_barrier_semaphore()
-    for other in far + near:
-        pl.semaphore_signal(barrier, inc=1, device_id={"sp": other * blocks + block}, device_id_type=MESH)
+
+    @pl.when(below)
+    def greet_below():
+        greet(barrier, at(-1, column))
+
+    @pl.when(above)
+    def greet_above():
+        greet(barrier, at(1, column))
+
+    greet(barrier, across)
     for partner in partners:
         pl.semaphore_signal(barrier, inc=1, device_id={"sp": group * blocks + partner}, device_id_type=MESH)
 
@@ -114,10 +134,74 @@
         for to in range(groups):
             head = to * per_group + j
             for i in range(3):
-                rows = wide[i, pl.ds(head, tokens, stride=heads), :]
-                send[to, j, i] = rows.astype(jnp.bfloat16)
-        if j == 0:
-            pl.semaphore_wait(barrier, groups - 1 + blocks - 1)
+                rows_of = wide[i, pl.ds(head, tokens, stride=heads), :]
+                send[to, j, i] = rows_of.astype(jnp.bfloat16)
+
+    def send_first(other):
+        outward(0, other, jnp.where(other // half == side, 0, 1)).start()
+
+    def tell_below(other):
+        @pl.when(below)
+        def tell():
+            greet(known.at[other], at(-1, column))
+
+    def tell_above(other):
+        @pl.when(above)
+        def tell():
+            greet(known.at[other], at(1, column))
+
+    def tell_across(other):
+        greet(known.at[other], across)
+
+    own(0).start()
+    pl.semaphore_wait(barrier, blocks + above.astype(jnp.int32) + below.astype(jnp.int32))
+
+    @pl.when(above)
+    def know_above():
+        other = at(1, column)
+        tell_below(other)
+        tell_across(other)
+        greet(known.at[across], other)
+
+    @pl.when(below)
+    def know_below():
+        tell_above(at(-1, column))
+
+    for step in range(1, rows):
+        @pl.when(row + step < rows)
+        def up():
+            other = at(step, column)
+            if step > 1:
+                pl.semaphore_wait(known.at[other], 1)
+                tell_below(other)
+                tell_across(other)
+            send_first(other)
+
+        @pl.when(row - step >= 0)
+        def down():
+            other = at(-step, column)
+            if step > 1:
+                pl.semaphore_wait(known.at[other], 1)
+                tell_above(other)
+            send_first(other)
+
+        if step == 1:
+            send_first(across)
+
+        @pl.when(row - step >= 0)
+        def down_across():
+            other = at(-step, 1 - column)
+            pl.semaphore_wait(known.at[other], 1)
+            tell_above(other)
+            send_first(other)
+
+        @pl.when(row + step < rows)
+        def up_across():
+            other = at(step, 1 - column)
+            pl.semaphore_wait(known.at[other], 1)
+            send_first(other)
+
+    for j in range(1, per_group):
         for other in far:
             outward(j, other, 1).start()
         for other in near:
@@ -198,6 +282,7 @@
             pltpu.SemaphoreType.DMA((per_group, blocks)),
             pltpu.SemaphoreType.DMA,
             pltpu.SemaphoreType.DMA,
+            pltpu.SemaphoreType.REGULAR((groups,)),
         ],
         compiler_params=pltpu.CompilerParams(collective_id=0, has_side_effects=True),
     )(queries, keys, values)

time: 34.4 us -> 33.7 us (0.980)
  Pallas kernels: 33.5 us -> 32.6 us
    pallas_call x1, Pallas kernels: 33.5 us -> 32.6 us  [shards(): pl.pallas_call(functools.partial(kernel, groups, blocks, per_group), out_...]
where the time goes in v1:
time: 33.7 us; the launch traced here: 33.4 us
  Pallas kernels  32.6 us (97%)
  local copies, waits for them, and re-layouts  0.72 us (2%)
    pallas_call x1, Pallas kernels, shards(): pl.pallas_call(functools.partial(kernel, groups, blocks, per_group), out_...  32.6 us
    unnamed x1, local copies, waits for them, and re-layouts  0.72 us

profile of v1, /device:TPU:0, one launch (start us, length us, event | category | flops | bytes accessed | tf_op | source)
XLA Modules:
  0.0 33.4 jit_solution(957164213360473592)
XLA Ops:
  0.0 32.6 %shard_map.37 = bf16[48,3072]{1,0:T(8,128)(2,1)S(1)} custom-call(bf16[48,24,128]{2,1,0:T(8,128)(2,1)} %q_hbm.1, bf16[48,24,128]{2,1,0:T(8,128)(2,1)} %k_hbm.1, bf16[48,24,128]{2,1,0:T(8,128)(2,1)} %v_hbm.1), custom_call_target="tpu_custom_call" | custom-call | tf_op jit(solution)/shard_map/pallas_call | solution.py:267
  32.6 0.7 %copy.5 = bf16[48,3072]{1,0:T(8,128)(2,1)} copy(bf16[48,3072]{1,0:T(8,128)(2,1)S(1)} %shard_map.37) | data formatting | bytes 589824

commit v2 on v0

v2 whole, which is shorter than its diff:
```python
import functools
import math

import jax
import jax.numpy as jnp
from jax import lax
from jax.experimental import pallas as pl
from jax.experimental.pallas import tpu as pltpu
from jax.sharding import PartitionSpec as P

MESH = pl.DeviceIdType.MESH
UNROLLED = 4


def kernel(
    owners, per_owner, size,
    q_hbm, k_hbm, v_hbm, landed,
    raw, wide, send, held, result,
    in_sem, send_sem, recv_sem, query_sem, back_sem, home_sem,
):
    me = lax.axis_index("sp")
    tokens, heads, width = q_hbm.shape
    first, half = (size - owners) // 2, owners // 2
    side = me // (size // 2)
    mine = me - first
    owner = jnp.logical_and(mine >= 0, mine < owners)
    last = per_owner - 1
    chunks = size // half

    loads = [
        pltpu.make_async_copy(src, raw.at[i], in_sem.at[i])
        for i, src in enumerate((k_hbm, v_hbm, q_hbm))
    ]
    for load in loads:
        load.start()

    barrier = pltpu.get_barrier_semaphore()

    @pl.when(owner)
    def greet():
        for step in range(1, size):
            other = lax.rem(me + step, size)
            pl.semaphore_signal(barrier, inc=1, device_id={"sp": other}, device_id_type=MESH)

    for i, load in enumerate(loads):
        load.wait()
        wide[i] = raw[i].astype(jnp.float32).reshape(tokens * heads, width)

    spot = lax.rem(mine + size, half)
    far = [(1 - side) * half + lax.rem(spot + step, half) for step in range(half)]
    near = [side * half + lax.rem(spot + step, half) for step in range(half)]

    def outward(j, to, parts, semaphore):
        return pltpu.make_async_remote_copy(
            src_ref=send.at[j, to, parts],
            dst_ref=held.at[j, me, parts],
            send_sem=send_sem,
            recv_sem=semaphore,
            device_id={"sp": first + to},
            device_id_type=MESH,
        )

    def own(j, parts, semaphore):
        return pltpu.make_async_copy(send.at[j, mine, parts], held.at[j, me, parts], semaphore)

    def spread(j, parts, semaphore, over=True, around=True):
        for step in range(half):
            if over:
                outward(j, far[step], parts, semaphore).start()
            if around and step > 0:
                outward(j, near[step], parts, semaphore).start()
        if around:
            @pl.when(owner)
            def keep():
                own(j, parts, semaphore).start()

            @pl.when(jnp.logical_not(owner))
            def give():
                outward(j, near[0], parts, semaphore).start()

    asking = pl.ds(2, 1), query_sem.at[me // half]

    for j in range(per_owner):
        for to in range(owners):
            head = to * per_owner + j
            for i in range(3):
                rows = wide[i, pl.ds(head, tokens, stride=heads), :]
                send[j, to, i] = rows.astype(jnp.bfloat16)
        if j == 0:
            @pl.when(owner)
            def meet():
                pl.semaphore_wait(barrier, owners - 1)

            @pl.when(jnp.logical_not(owner))
            def see():
                pl.semaphore_wait(barrier, owners)

        if j < last:
            spread(j, pl.ds(0, 3), recv_sem.at[j])

    @pl.when(jnp.logical_not(owner))
    def ask():
        spread(last, *asking)

    spread(last, pl.ds(0, 2), recv_sem.at[last])

    @pl.when(owner)
    def ask_near():
        spread(last, *asking, over=False)

    def columns(j):
        return pl.ds(pl.multiple_of((mine * per_owner + j) * width, width), width)

    def back(j, other):
        return pltpu.make_async_remote_copy(
            src_ref=result.at[j, other],
            dst_ref=landed.at[:, columns(j)],
            send_sem=back_sem,
            recv_sem=home_sem,
            device_id={"sp": other},
            device_id_type=MESH,
        )

    def own_back(j):
        return pltpu.make_async_copy(result.at[j, me], landed.at[:, columns(j)], home_sem)

    factor = math.log2(math.e) / math.sqrt(width)

    middle = chunks // 2

    def chunk_of(place):
        lower = jnp.where(place == 0, 0, jnp.where(place <= chunks - middle, chunks - place, place - chunks + middle))
        upper = jnp.where(place < middle, place, chunks + middle - 1 - place)
        return jnp.where(side > 0, upper, lower)

    def attend(j, place):
        chunk = chunk_of(place)
        picked = pl.ds(chunk * half, half)
        if j == last:
            asked = held.at[j, picked, pl.ds(2, 1)]
            pltpu.make_async_copy(asked, asked, query_sem.at[chunk]).wait()
        keys = held[j, :, 0].reshape(-1, width)
        values = held[j, :, 1].reshape(-1, width)
        queries = held[j, picked, 2].reshape(half * tokens, width)
        scores = lax.dot_general(
            queries, keys, (((1,), (1,)), ((), ())), preferred_element_type=jnp.float32
        )
        top = jnp.max(scores, axis=-1, keepdims=True)
        weights = jnp.exp2((scores - top) * factor)
        total = jnp.sum(weights, axis=-1, keepdims=True)
        attended = jnp.dot(
            weights.astype(jnp.bfloat16), values, preferred_element_type=jnp.float32
        ) / total
        result[j, picked] = attended.astype(jnp.bfloat16).reshape(half, tokens, width)

    def deliver(j, place):
        chunk = chunk_of(place)
        for step in range(half):
            other = chunk * half + step
            if isinstance(place, int) and place < chunks - 1:
                back(j, other).start()
            else:
                @pl.when(other != me)
                def give():
                    back(j, other).start()

    def early(j):
        attend(j, 0)
        deliver(j, 0)
        if j == 0:
            spread(last, *asking, around=False)

    def late(j, place):
        attend(j, place)
        deliver(j, place)

    @pl.when(owner)
    def work():
        for j in range(per_owner):
            whole = held.at[j] if j < last else held.at[j, :, pl.ds(0, 2)]
            pltpu.make_async_copy(whole, whole, recv_sem.at[j]).wait()
            early(j)
            if chunks > UNROLLED:
                pl.loop(1, chunks)(functools.partial(late, j))
            else:
                if j == last and last > 0:
                    deliver(last - 1, 1)
                for place in range(1, chunks):
                    attend(j, place)
                    if place > 1 or j != last - 1:
                        deliver(j, place)
            own_back(j).start()
        sent = send.at[:, pl.ds(0, owners - 1)]
        pltpu.make_async_copy(sent, sent, send_sem).wait()
        given = result.at[:, pl.ds(0, size - 1)]
        pltpu.make_async_copy(given, given, back_sem).wait()

    @pl.when(jnp.logical_not(owner))
    def rest():
        pltpu.make_async_copy(send, send, send_sem).wait()

    pltpu.make_async_copy(landed, landed, home_sem).wait()


def shards(queries, keys, values):
    tokens, heads, width = queries.shape
    size = lax.axis_size("sp")
    owners = math.gcd(heads, size // 2)
    per_owner = heads // owners
    kind = queries.dtype
    return pl.pallas_call(
        functools.partial(kernel, owners, per_owner, size),
        out_shape=pltpu.VMEM((tokens, heads * width), kind),
        in_specs=[pl.BlockSpec(memory_space=pl.ANY)] * 3,
        out_specs=pl.BlockSpec(memory_space=pltpu.VMEM),
        scratch_shapes=[
            pltpu.VMEM((3, tokens, heads, width), kind),
            pltpu.VMEM((3, tokens * heads, width), jnp.float32),
            pltpu.VMEM((per_owner, owners, 3, tokens, width), kind),
            pltpu.VMEM((per_owner, size, 3, tokens, width), kind),
            pltpu.VMEM((per_owner, size, tokens, width), kind),
            pltpu.SemaphoreType.DMA((3,)),
            pltpu.SemaphoreType.DMA,
            pltpu.SemaphoreType.DMA((per_owner,)),
            pltpu.SemaphoreType.DMA((2 * size // owners,)),
            pltpu.SemaphoreType.DMA,
            pltpu.SemaphoreType.DMA,
        ],
        compiler_params=pltpu.CompilerParams(collective_id=0, has_side_effects=True),
    )(queries, keys, values)


def solution(mesh):
    return jax.shard_map(
        shards,
        mesh=mesh,
        in_specs=(
            P(("dp", "sp"), None, None),
            P(("dp", "sp"), None, None),
            P(("dp", "sp"), None, None),
        ),
        out_specs=P(("dp", "sp"), None),
        check_vma=False,
    )
```

time: 34.4 us -> 31.1 us (0.904)
  Pallas kernels: 33.5 us -> 30.3 us
    pallas_call x1, Pallas kernels: 33.5 us -> 30.3 us  [shards(): pl.pallas_call(functools.partial(kernel, owners, per_owner, size), out_sh...]
where the time goes in v2:
time: 31.1 us; the launch traced here: 31 us
  Pallas kernels  30.3 us (97%)
  local copies, waits for them, and re-layouts  0.72 us (2%)
    pallas_call x1, Pallas kernels, shards(): pl.pallas_call(functools.partial(kernel, owners, per_owner, size), out_sh...  30.3 us
    unnamed x1, local copies, waits for them, and re-layouts  0.72 us

profile of v2, /device:TPU:0, one launch (start us, length us, event | category | flops | bytes accessed | tf_op | source)
XLA Modules:
  0.0 31.0 jit_solution(18069941118772019511)
XLA Ops:
  0.0 30.3 %shard_map.37 = bf16[48,3072]{1,0:T(8,128)(2,1)S(1)} custom-call(bf16[48,24,128]{2,1,0:T(8,128)(2,1)} %q_hbm.1, bf16[48,24,128]{2,1,0:T(8,128)(2,1)} %k_hbm.1, bf16[48,24,128]{2,1,0:T(8,128)(2,1)} %v_hbm.1), custom_call_target="tpu_custom_call" | custom-call | tf_op jit(solution)/shard_map/pallas_call | solution.py:211
  30.3 0.7 %copy.5 = bf16[48,3072]{1,0:T(8,128)(2,1)} copy(bf16[48,3072]{1,0:T(8,128)(2,1)S(1)} %shard_map.37) | data formatting | bytes 589824

commit v3 on v2

v3 whole, which is shorter than its diff:
```python
import functools
import math

import jax
import jax.numpy as jnp
from jax import lax
from jax.experimental import pallas as pl
from jax.experimental.pallas import tpu as pltpu
from jax.sharding import PartitionSpec as P

MESH = pl.DeviceIdType.MESH
UNROLLED = 4
ALL, PAIR, ASK = pl.ds(0, 3), pl.ds(0, 2), pl.ds(2, 1)


def kernel(
    owners, slots, size,
    q_hbm, k_hbm, v_hbm, landed,
    raw, wide, send, held, result,
    in_sem, send_sem, recv_sem, query_sem, back_sem, home_sem, near_sem,
):
    me = lax.axis_index("sp")
    tokens, _, width = q_hbm.shape
    first, half = (size - owners) // 2, owners // 2
    side = me // (size // 2)
    mine = me - first
    owner = jnp.logical_and(mine >= 0, mine < owners)
    outer = jnp.logical_not(owner)
    last = slots - 1
    chunks = size // half

    def load(j, i, src):
        return pltpu.make_async_copy(
            src.at[:, pl.ds(j * owners, owners), :], raw.at[j, i], in_sem.at[j]
        )

    for j in range(slots):
        for i, src in enumerate((k_hbm, v_hbm, q_hbm)):
            load(j, i, src).start()

    barrier = pltpu.get_barrier_semaphore()

    def greet(semaphore, other):
        pl.semaphore_signal(semaphore, inc=1, device_id={"sp": other}, device_id_type=MESH)

    spot = lax.rem(mine + size, half)
    far = [(1 - side) * half + lax.rem(spot + step, half) for step in range(half)]
    near = [side * half + lax.rem(spot + step, half) for step in range(half)]

    low = side == 0
    mates = range(0, first, half)

    @pl.when(owner)
    def enter():
        for to in far:
            greet(barrier, first + to)
        for other in range(first):
            greet(barrier, size - 1 - other)

        @pl.when(low)
        def enter_low():
            for other in range(first):
                greet(barrier, other)

    @pl.when(jnp.logical_and(outer, low))
    def enter_outer():
        greet(barrier, first + spot)

    def outward(j, to, parts, semaphore):
        return pltpu.make_async_remote_copy(
            src_ref=send.at[j, to, parts],
            dst_ref=held.at[j, me, parts],
            send_sem=send_sem,
            recv_sem=semaphore,
            device_id={"sp": first + to},
            device_id_type=MESH,
        )

    def own(j, parts, semaphore):
        return pltpu.make_async_copy(send.at[j, mine, parts], held.at[j, me, parts], semaphore)

    def asking():
        return query_sem.at[me // half]

    def spread(targets, j, parts, semaphore):
        for to in targets:
            outward(j, to, parts, semaphore).start()

    mixed = [to for pair in zip(far, near) for to in pair]
    crew = jnp.where(owner, half + jnp.where(low, len(mates), 0), jnp.where(low, half, owners))
    for j in range(slots):
        pltpu.make_async_copy(raw.at[j], raw.at[j], in_sem.at[j]).wait()
        for i in range(3):
            wide[j, i] = raw[j, i].astype(jnp.float32).reshape(tokens * owners, width)
        for to in range(owners):
            for i in range(3):
                rows = wide[j, i, pl.ds(to, tokens, stride=owners), :]
                send[j, to, i] = rows.astype(jnp.bfloat16)
        if j == 0:
            pl.semaphore_wait(barrier, crew)

        @pl.when(owner)
        def cross():
            if j == 0:
                greet(near_sem, first + far[0])
            spread(far, j, PAIR if j == last else ALL, recv_sem.at[j])

            @pl.when(low)
            def tell():
                if j == 0:
                    for mate in mates:
                        greet(near_sem, mate + spot)

        @pl.when(jnp.logical_and(outer, low))
        def give_low():
            if j == 0:
                spread(near, j, ALL, recv_sem.at[j])
                pl.semaphore_wait(near_sem, 1)
                spread(far, j, ALL, recv_sem.at[j])
            elif j < last:
                spread(mixed, j, ALL, recv_sem.at[j])
            else:
                spread(mixed, j, ASK, asking())
                spread(mixed, j, PAIR, recv_sem.at[j])

        @pl.when(jnp.logical_and(outer, jnp.logical_not(low)))
        def give_high():
            spread(mixed, j, PAIR if j == last else ALL, recv_sem.at[j])
            if j == last:
                spread(mixed, j, ASK, asking())

    @pl.when(owner)
    def around():
        pl.semaphore_wait(near_sem, 1)
        for j in range(slots):
            spread(near[1:], j, PAIR if j == last else ALL, recv_sem.at[j])
            own(j, PAIR if j == last else ALL, recv_sem.at[j]).start()
        spread(near[1:], last, ASK, asking())
        own(last, ASK, asking()).start()

    def columns(j):
        return pl.ds(pl.multiple_of((j * owners + mine) * width, width), width)

    def back(j, other):
        return pltpu.make_async_remote_copy(
            src_ref=result.at[j, other],
            dst_ref=landed.at[:, columns(j)],
            send_sem=back_sem,
            recv_sem=home_sem,
            device_id={"sp": other},
            device_id_type=MESH,
        )

    def own_back(j):
        return pltpu.make_async_copy(result.at[j, me], landed.at[:, columns(j)], home_sem)

    factor = math.log2(math.e) / math.sqrt(width)

    def arrived(j):
        whole = held.at[j, :, PAIR] if j == last else held.at[j]
        pltpu.make_async_copy(whole, whole, recv_sem.at[j]).wait()

    def attend(j, chunk):
        picked = pl.ds(chunk * half, half)
        if j == last:
            asked = held.at[j, picked, ASK]
            pltpu.make_async_copy(asked, asked, query_sem.at[chunk]).wait()
        keys = held[j, :, 0].reshape(-1, width)
        values = held[j, :, 1].reshape(-1, width)
        queries = held[j, picked, 2].reshape(half * tokens, width)
        scores = lax.dot_general(
            queries, keys, (((1,), (1,)), ((), ())), preferred_element_type=jnp.float32
        )
        top = jnp.max(scores, axis=-1, keepdims=True)
        weights = jnp.exp2((scores - top) * factor)
        total = jnp.sum(weights, axis=-1, keepdims=True)
        attended = jnp.dot(
            weights.astype(jnp.bfloat16), values, preferred_element_type=jnp.float32
        ) / total
        result[j, picked] = attended.astype(jnp.bfloat16).reshape(half, tokens, width)

    def deliver(j, chunk, steps=None):
        for step in steps or range(half):
            back(j, chunk * half + step).start()

    def deliver_around(j, chunk):
        for step in range(half):
            other = chunk * half + step

            @pl.when(other != me)
            def give():
                back(j, other).start()

        own_back(j).start()

    inner = first // half
    opposite, beside = inner + 1 - side, inner + side
    head, tail = 0, chunks - 1

    def ask_across():
        spread(far, last, ASK, asking())

    def remaining():
        for start, stop in ((1, inner), (inner + 2, chunks - 1)):
            for j in range(slots if stop > start else 0):
                @pl.loop(start, stop)
                def step(chunk):
                    attend(j, chunk)
                    deliver(j, chunk)

    @pl.when(owner)
    def work():
        second = jnp.where(low, tail, opposite)
        third = jnp.where(low, opposite, tail)
        for j in range(slots):
            arrived(j)
            attend(j, head)
            deliver(j, head)
            if j == 0:
                ask_across()
            if j == 1:
                @pl.when(jnp.logical_not(low))
                def release_rest():
                    deliver(0, opposite, range(0, half))
            if j == last and last > 0:
                deliver(last - 1, second)
            attend(j, second)
            if j == 0:
                pl.when(low)(functools.partial(deliver, j, second))

                @pl.when(jnp.logical_not(low))
                def deliver_some():
                    pass
            elif j != last - 1:
                deliver(j, second)
            attend(j, third)
            deliver(j, third)
            attend(j, beside)
            deliver_around(j, beside)
        remaining()

        sent = send.at[:, pl.ds(0, owners - 1)]
        pltpu.make_async_copy(sent, sent, send_sem).wait()
        given = result.at[:, pl.ds(0, size - 1)]
        pltpu.make_async_copy(given, given, back_sem).wait()

    @pl.when(outer)
    def rest():
        pltpu.make_async_copy(send, send, send_sem).wait()

    pltpu.make_async_copy(landed, landed, home_sem).wait()


def shards(queries, keys, values):
    tokens, heads, width = queries.shape
    size = lax.axis_size("sp")
    owners = math.gcd(heads, size // 2)
    slots = heads // owners
    kind = queries.dtype
    return pl.pallas_call(
        functools.partial(kernel, owners, slots, size),
        out_shape=pltpu.VMEM((tokens, heads * width), kind),
        in_specs=[pl.BlockSpec(memory_space=pl.ANY)] * 3,
        out_specs=pl.BlockSpec(memory_space=pltpu.VMEM),
        scratch_shapes=[
            pltpu.VMEM((slots, 3, tokens, owners, width), kind),
            pltpu.VMEM((slots, 3, tokens * owners, width), jnp.float32),
            pltpu.VMEM((slots, owners, 3, tokens, width), kind),
            pltpu.VMEM((slots, size, 3, tokens, width), kind),
            pltpu.VMEM((slots, size, tokens, width), kind),
            pltpu.SemaphoreType.DMA((slots,)),
            pltpu.SemaphoreType.DMA,
            pltpu.SemaphoreType.DMA((slots,)),
            pltpu.SemaphoreType.DMA((2 * size // owners,)),
            pltpu.SemaphoreType.DMA,
            pltpu.SemaphoreType.DMA,
            pltpu.SemaphoreType.REGULAR,
        ],
        compiler_params=pltpu.CompilerParams(collective_id=0, has_side_effects=True),
    )(queries, keys, values)


def solution(mesh):
    return jax.shard_map(
        shards,
        mesh=mesh,
        in_specs=(
            P(("dp", "sp"), None, None),
            P(("dp", "sp"), None, None),
            P(("dp", "sp"), None, None),
        ),
        out_specs=P(("dp", "sp"), None),
        check_vma=False,
    )
```

time: 31.1 us -> 30.5 us (0.981)
  Pallas kernels: 30.3 us -> 29.6 us
    pallas_call x1, Pallas kernels: 30.3 us -> 29.6 us  [shards(): pl.pallas_call(functools.partial(kernel, owners, slots, size), out_shape=...]
where the time goes in v3:
time: 30.5 us; the launch traced here: 30.4 us
  Pallas kernels  29.6 us (97%)
  local copies, waits for them, and re-layouts  0.72 us (2%)
    pallas_call x1, Pallas kernels, shards(): pl.pallas_call(functools.partial(kernel, owners, slots, size), out_shape=...  29.6 us
    unnamed x1, local copies, waits for them, and re-layouts  0.72 us

profile of v3, /device:TPU:0, one launch (start us, length us, event | category | flops | bytes accessed | tf_op | source)
XLA Modules:
  0.0 30.4 jit_solution(17031834180473147268)
XLA Ops:
  0.0 29.6 %shard_map.37 = bf16[48,3072]{1,0:T(8,128)(2,1)S(1)} custom-call(bf16[48,24,128]{2,1,0:T(8,128)(2,1)} %q_hbm.1, bf16[48,24,128]{2,1,0:T(8,128)(2,1)} %k_hbm.1, bf16[48,24,128]{2,1,0:T(8,128)(2,1)} %v_hbm.1), custom_call_target="tpu_custom_call" | custom-call | tf_op jit(solution)/shard_map/pallas_call | solution.py:260
  29.6 0.7 %copy.5 = bf16[48,3072]{1,0:T(8,128)(2,1)} copy(bf16[48,3072]{1,0:T(8,128)(2,1)S(1)} %shard_map.37) | data formatting | bytes 589824

commit v4 on v3

--- a/solution.py
+++ b/solution.py
@@ -9,7 +9,6 @@
 from jax.sharding import PartitionSpec as P
 
 MESH = pl.DeviceIdType.MESH
-UNROLLED = 4
 ALL, PAIR, ASK = pl.ds(0, 3), pl.ds(0, 2), pl.ds(2, 1)
 
 
@@ -160,14 +159,15 @@
         whole = held.at[j, :, PAIR] if j == last else held.at[j]
         pltpu.make_async_copy(whole, whole, recv_sem.at[j]).wait()
 
-    def attend(j, chunk):
-        picked = pl.ds(chunk * half, half)
-        if j == last:
-            asked = held.at[j, picked, ASK]
+    def attend(j, chunk, steps=None):
+        steps = steps or range(half)
+        if j == last and steps[0] == 0:
+            asked = held.at[j, pl.ds(chunk * half, half), ASK]
             pltpu.make_async_copy(asked, asked, query_sem.at[chunk]).wait()
+        picked = pl.ds(chunk * half + steps[0], len(steps))
         keys = held[j, :, 0].reshape(-1, width)
         values = held[j, :, 1].reshape(-1, width)
-        queries = held[j, picked, 2].reshape(half * tokens, width)
+        queries = held[j, picked, 2].reshape(len(steps) * tokens, width)
         scores = lax.dot_general(
             queries, keys, (((1,), (1,)), ((), ())), preferred_element_type=jnp.float32
         )
@@ -177,7 +177,7 @@
         attended = jnp.dot(
             weights.astype(jnp.bfloat16), values, preferred_element_type=jnp.float32
         ) / total
-        result[j, picked] = attended.astype(jnp.bfloat16).reshape(half, tokens, width)
+        result[j, picked] = attended.astype(jnp.bfloat16).reshape(len(steps), tokens, width)
 
     def deliver(j, chunk, steps=None):
         for step in steps or range(half):
@@ -193,7 +193,7 @@
 
         own_back(j).start()
 
-    inner = first // half
+    inner, wing = first // half, half // 2
     opposite, beside = inner + 1 - side, inner + side
     head, tail = 0, chunks - 1
 
@@ -212,31 +212,38 @@
     def work():
         second = jnp.where(low, tail, opposite)
         third = jnp.where(low, opposite, tail)
+        high = jnp.logical_not(low)
+        front, rear = range(wing), range(wing, half)
         for j in range(slots):
             arrived(j)
-            attend(j, head)
-            deliver(j, head)
-            if j == 0:
-                ask_across()
+            for steps in (front, rear) if j == last else (range(half),):
+                attend(j, head, steps)
+                deliver(j, head, steps)
+            if j == 0:
+                pl.when(high)(ask_across)
             if j == 1:
-                @pl.when(jnp.logical_not(low))
-                def release_rest():
-                    deliver(0, opposite, range(0, half))
-            if j == last and last > 0:
-                deliver(last - 1, second)
+                pl.when(high)(functools.partial(deliver, 0, opposite))
+            if j == last:
+                pl.when(low)(functools.partial(deliver, last - 1, tail))
+                pl.when(high)(functools.partial(deliver, last - 1, opposite, front))
             attend(j, second)
-            if j == 0:
-                pl.when(low)(functools.partial(deliver, j, second))
-
-                @pl.when(jnp.logical_not(low))
-                def deliver_some():
-                    pass
-            elif j != last - 1:
-                deliver(j, second)
+            if j == last:
+                deliver(j, second, front)
+                pl.when(high)(functools.partial(deliver, last - 1, opposite, rear))
+                deliver(j, second, rear)
             attend(j, third)
-            deliver(j, third)
+            if j == 0:
+                pl.when(high)(functools.partial(deliver, j, tail))
+            else:
+                deliver(j, third)
             attend(j, beside)
             deliver_around(j, beside)
+            if j == 0:
+                @pl.when(low)
+                def open_low():
+                    ask_across()
+                    deliver(0, tail)
+                    deliver(0, opposite)
         remaining()
 
         sent = send.at[:, pl.ds(0, owners - 1)]

time: 30.5 us -> 30.4 us (level)
  no operation moved by 1% of the time
where the time goes in v4:
time: 30.4 us; the launch traced here: 30.3 us
  Pallas kernels  29.6 us (97%)
  local copies, waits for them, and re-layouts  0.72 us (2%)
    pallas_call x1, Pallas kernels, shards(): pl.pallas_call(functools.partial(kernel, owners, slots, size), out_shape=...  29.6 us
    unnamed x1, local copies, waits for them, and re-layouts  0.72 us

profile of v4, /device:TPU:0, one launch (start us, length us, event | category | flops | bytes accessed | tf_op | source)
XLA Modules:
  0.0 30.3 jit_solution(11931321278827115824)
XLA Ops:
  0.0 29.6 %shard_map.37 = bf16[48,3072]{1,0:T(8,128)(2,1)S(1)} custom-call(bf16[48,24,128]{2,1,0:T(8,128)(2,1)} %q_hbm.1, bf16[48,24,128]{2,1,0:T(8,128)(2,1)} %k_hbm.1, bf16[48,24,128]{2,1,0:T(8,128)(2,1)} %v_hbm.1), custom_call_target="tpu_custom_call" | custom-call | tf_op jit(solution)/shard_map/pallas_call | solution.py:267
  29.6 0.7 %copy.5 = bf16[48,3072]{1,0:T(8,128)(2,1)} copy(bf16[48,3072]{1,0:T(8,128)(2,1)S(1)} %shard_map.37) | data formatting | bytes 589824

commit v5 on v4

--- a/solution.py
+++ b/solution.py
@@ -181,6 +181,7 @@
 
     def deliver(j, chunk, steps=None):
         for step in steps or range(half):
+            step = step if chunk is head else step ^ 1
             back(j, chunk * half + step).start()
 
     def deliver_around(j, chunk):

time: 30.4 us -> 30.4 us (level)
  no operation moved by 1% of the time
where the time goes in v5:
time: 30.4 us; the launch traced here: 30.3 us
  Pallas kernels  29.6 us (97%)
  local copies, waits for them, and re-layouts  0.72 us (2%)
    pallas_call x1, Pallas kernels, shards(): pl.pallas_call(functools.partial(kernel, owners, slots, size), out_shape=...  29.6 us
    unnamed x1, local copies, waits for them, and re-layouts  0.72 us

profile of v5, /device:TPU:0, one launch (start us, length us, event | category | flops | bytes accessed | tf_op | source)
XLA Modules:
  0.0 30.3 jit_solution(9335764357882048261)
XLA Ops:
  0.0 29.6 %shard_map.37 = bf16[48,3072]{1,0:T(8,128)(2,1)S(1)} custom-call(bf16[48,24,128]{2,1,0:T(8,128)(2,1)} %q_hbm.1, bf16[48,24,128]{2,1,0:T(8,128)(2,1)} %k_hbm.1, bf16[48,24,128]{2,1,0:T(8,128)(2,1)} %v_hbm.1), custom_call_target="tpu_custom_call" | custom-call | tf_op jit(solution)/shard_map/pallas_call | solution.py:268
  29.6 0.7 %copy.5 = bf16[48,3072]{1,0:T(8,128)(2,1)} copy(bf16[48,3072]{1,0:T(8,128)(2,1)S(1)} %shard_map.37) | data formatting | bytes 589824

commit v6 on v5

--- a/solution.py
+++ b/solution.py
@@ -75,6 +75,9 @@
             device_id_type=MESH,
         )
 
+    def landing(j):
+        return recv_sem.at[jnp.where(me < half, slots, last) if j == last else j]
+
     def own(j, parts, semaphore):
         return pltpu.make_async_copy(send.at[j, mine, parts], held.at[j, me, parts], semaphore)
 
@@ -102,7 +105,7 @@
         def cross():
             if j == 0:
                 greet(near_sem, first + far[0])
-            spread(far, j, PAIR if j == last else ALL, recv_sem.at[j])
+            spread(far, j, PAIR if j == last else ALL, landing(j))
 
             @pl.when(low)
             def tell():
@@ -120,11 +123,11 @@
                 spread(mixed, j, ALL, recv_sem.at[j])
             else:
                 spread(mixed, j, ASK, asking())
-                spread(mixed, j, PAIR, recv_sem.at[j])
+                spread(mixed, j, PAIR, landing(j))
 
         @pl.when(jnp.logical_and(outer, jnp.logical_not(low)))
         def give_high():
-            spread(mixed, j, PAIR if j == last else ALL, recv_sem.at[j])
+            spread(mixed, j, PAIR if j == last else ALL, landing(j))
             if j == last:
                 spread(mixed, j, ASK, asking())
 
@@ -132,8 +135,8 @@
     def around():
         pl.semaphore_wait(near_sem, 1)
         for j in range(slots):
-            spread(near[1:], j, PAIR if j == last else ALL, recv_sem.at[j])
-            own(j, PAIR if j == last else ALL, recv_sem.at[j]).start()
+            spread(near[1:], j, PAIR if j == last else ALL, landing(j))
+            own(j, PAIR if j == last else ALL, landing(j)).start()
         spread(near[1:], last, ASK, asking())
         own(last, ASK, asking()).start()
 
@@ -156,18 +159,48 @@
     factor = math.log2(math.e) / math.sqrt(width)
 
     def arrived(j):
-        whole = held.at[j, :, PAIR] if j == last else held.at[j]
+        whole = held.at[j, pl.ds(half, size - half), PAIR] if j == last else held.at[j]
         pltpu.make_async_copy(whole, whole, recv_sem.at[j]).wait()
 
-    def attend(j, chunk, steps=None):
-        steps = steps or range(half)
-        if j == last and steps[0] == 0:
-            asked = held.at[j, pl.ds(chunk * half, half), ASK]
+    def product(queries, keys):
+        return lax.dot_general(
+            queries, keys, (((1,), (1,)), ((), ())), preferred_element_type=jnp.float32
+        )
+
+    def attend_split(j, chunk):
+        asked = held.at[j, pl.ds(chunk * half, half), ASK]
+        pltpu.make_async_copy(asked, asked, query_sem.at[chunk]).wait()
+        queries = held[j, pl.ds(chunk * half, half), 2].reshape(half * tokens, width)
+        scores = product(queries, held[j, pl.ds(half, size - half), 0].reshape(-1, width))
+        early = jnp.max(scores, axis=-1, keepdims=True)
+        weights = jnp.exp2((scores - early) * factor)
+        total = jnp.sum(weights, axis=-1, keepdims=True)
+        values = held[j, pl.ds(half, size - half), 1].reshape(-1, width)
+        attended = jnp.dot(weights.astype(jnp.bfloat16), values, preferred_element_type=jnp.float32)
+
+        rest = held.at[j, pl.ds(0, half), PAIR]
+        pltpu.make_async_copy(rest, rest, recv_sem.at[slots]).wait()
+        scores = product(queries, held[j, pl.ds(0, half), 0].reshape(-1, width))
+        top = jnp.maximum(early, jnp.max(scores, axis=-1, keepdims=True))
+        weights = jnp.exp2((scores - top) * factor)
+        scale = jnp.exp2((early - top) * factor)
+        total = total * scale + jnp.sum(weights, axis=-1, keepdims=True)
+        values = held[j, pl.ds(0, half), 1].reshape(-1, width)
+        attended = attended * scale + jnp.dot(
+            weights.astype(jnp.bfloat16), values, preferred_element_type=jnp.float32
+        )
+        result[j, pl.ds(chunk * half, half)] = (
+            (attended / total).astype(jnp.bfloat16).reshape(half, tokens, width)
+        )
+
+    def attend(j, chunk):
+        picked = pl.ds(chunk * half, half)
+        if j == last:
+            asked = held.at[j, picked, ASK]
             pltpu.make_async_copy(asked, asked, query_sem.at[chunk]).wait()
-        picked = pl.ds(chunk * half + steps[0], len(steps))
         keys = held[j, :, 0].reshape(-1, width)
         values = held[j, :, 1].reshape(-1, width)
-        queries = held[j, picked, 2].reshape(len(steps) * tokens, width)
+        queries = held[j, picked, 2].reshape(half * tokens, width)
         scores = lax.dot_general(
             queries, keys, (((1,), (1,)), ((), ())), preferred_element_type=jnp.float32
         )
@@ -177,7 +210,7 @@
         attended = jnp.dot(
             weights.astype(jnp.bfloat16), values, preferred_element_type=jnp.float32
         ) / total
-        result[j, picked] = attended.astype(jnp.bfloat16).reshape(len(steps), tokens, width)
+        result[j, picked] = attended.astype(jnp.bfloat16).reshape(half, tokens, width)
 
     def deliver(j, chunk, steps=None):
         for step in steps or range(half):
@@ -217,9 +250,8 @@
         front, rear = range(wing), range(wing, half)
         for j in range(slots):
             arrived(j)
-            for steps in (front, rear) if j == last else (range(half),):
-                attend(j, head, steps)
-                deliver(j, head, steps)
+            (attend_split if j == last else attend)(j, head)
+            deliver(j, head)
             if j == 0:
                 pl.when(high)(ask_across)
             if j == 1:
@@ -278,7 +310,7 @@
             pltpu.VMEM((slots, size, tokens, width), kind),
             pltpu.SemaphoreType.DMA((slots,)),
             pltpu.SemaphoreType.DMA,
-            pltpu.SemaphoreType.DMA((slots,)),
+            pltpu.SemaphoreType.DMA((slots + 1,)),
             pltpu.SemaphoreType.DMA((2 * size // owners,)),
             pltpu.SemaphoreType.DMA,
             pltpu.SemaphoreType.DMA,

time: 30.4 us -> 30.5 us (level)
  no operation moved by 1% of the time
where the time goes in v6:
time: 30.5 us; the launch traced here: 30.4 us
  Pallas kernels  29.6 us (97%)
  local copies, waits for them, and re-layouts  0.72 us (2%)
    pallas_call x1, Pallas kernels, shards(): pl.pallas_call(functools.partial(kernel, owners, slots, size), out_shape=...  29.6 us
    unnamed x1, local copies, waits for them, and re-layouts  0.72 us

profile of v6, /device:TPU:0, one launch (start us, length us, event | category | flops | bytes accessed | tf_op | source)
XLA Modules:
  0.0 30.4 jit_solution(13748142889010697686)
XLA Ops:
  0.0 29.6 %shard_map.37 = bf16[48,3072]{1,0:T(8,128)(2,1)S(1)} custom-call(bf16[48,24,128]{2,1,0:T(8,128)(2,1)} %q_hbm.1, bf16[48,24,128]{2,1,0:T(8,128)(2,1)} %k_hbm.1, bf16[48,24,128]{2,1,0:T(8,128)(2,1)} %v_hbm.1), custom_call_target="tpu_custom_call" | custom-call | tf_op jit(solution)/shard_map/pallas_call | solution.py:300
  29.6 0.7 %copy.5 = bf16[48,3072]{1,0:T(8,128)(2,1)} copy(bf16[48,3072]{1,0:T(8,128)(2,1)S(1)} %shard_map.37) | data formatting | bytes 589824

commit v7 on v5

--- a/solution.py
+++ b/solution.py
@@ -16,7 +16,7 @@
     owners, slots, size,
     q_hbm, k_hbm, v_hbm, landed,
     raw, wide, send, held, result,
-    in_sem, send_sem, recv_sem, query_sem, back_sem, home_sem, near_sem,
+    in_sem, send_sem, recv_sem, query_sem, back_sem, home_sem, near_sem, cross_sem,
 ):
     me = lax.axis_index("sp")
     tokens, _, width = q_hbm.shape
@@ -49,10 +49,26 @@
     low = side == 0
     mates = range(0, first, half)
 
+    wing = half // 2
+    lead = jnp.logical_and(spot < wing, side > 0)
+    lower = [(1 - side) * half + lax.rem(spot + step, wing) for step in range(wing)]
+    upper = [to + wing for to in lower]
+    beyond = first + side * half + lax.rem(spot + wing, half)
+
     @pl.when(owner)
     def enter():
-        for to in far:
+        for to in upper:
             greet(barrier, first + to)
+
+        @pl.when(jnp.logical_or(spot < wing, side > 0))
+        def enter_lower():
+            for to in lower:
+                greet(barrier, first + to)
+
+        @pl.when(lead)
+        def enter_lead():
+            greet(barrier, beyond)
+
         for other in range(first):
             greet(barrier, size - 1 - other)
 
@@ -86,7 +102,7 @@
             outward(j, to, parts, semaphore).start()
 
     mixed = [to for pair in zip(far, near) for to in pair]
-    crew = jnp.where(owner, half + jnp.where(low, len(mates), 0), jnp.where(low, half, owners))
+    crew = jnp.where(owner, jnp.where(lead, wing, half) + jnp.where(low, len(mates), jnp.where(lead, 0, 1)), jnp.where(low, half, owners))
     for j in range(slots):
         pltpu.make_async_copy(raw.at[j], raw.at[j], in_sem.at[j]).wait()
         for i in range(3):
@@ -100,15 +116,34 @@
 
         @pl.when(owner)
         def cross():
-            if j == 0:
+            def tell():
                 greet(near_sem, first + far[0])
-            spread(far, j, PAIR if j == last else ALL, recv_sem.at[j])
-
-            @pl.when(low)
-            def tell():
-                if j == 0:
+
+                @pl.when(low)
+                def tell_mates():
                     for mate in mates:
                         greet(near_sem, mate + spot)
+
+            if j == 0:
+                @pl.when(lead)
+                def start_lead():
+                    spread(lower, 0, ALL, recv_sem.at[0])
+
+                @pl.when(jnp.logical_not(lead))
+                def start_rest():
+                    pl.when(jnp.logical_not(low))(functools.partial(greet, cross_sem, beyond))
+                    tell()
+                    spread(far, 0, ALL, recv_sem.at[0])
+
+            if j == 1:
+                @pl.when(lead)
+                def follow():
+                    pl.semaphore_wait(cross_sem, 1)
+                    tell()
+                    spread(upper, 0, ALL, recv_sem.at[0])
+
+            if j > 0:
+                spread(far, j, PAIR if j == last else ALL, recv_sem.at[j])
 
         @pl.when(jnp.logical_and(outer, low))
         def give_low():
@@ -194,7 +229,7 @@
 
         own_back(j).start()
 
-    inner, wing = first // half, half // 2
+    inner = first // half
     opposite, beside = inner + 1 - side, inner + side
     head, tail = 0, chunks - 1
 
@@ -283,6 +318,7 @@
             pltpu.SemaphoreType.DMA,
             pltpu.SemaphoreType.DMA,
             pltpu.SemaphoreType.REGULAR,
+            pltpu.SemaphoreType.REGULAR,
         ],
         compiler_params=pltpu.CompilerParams(collective_id=0, has_side_effects=True),
     )(queries, keys, values)

time: 30.4 us -> 30.4 us (level)
  no operation moved by 1% of the time
where the time goes in v7:
time: 30.4 us; the launch traced here: 30.3 us
  Pallas kernels  29.6 us (97%)
  local copies, waits for them, and re-layouts  0.72 us (2%)
    pallas_call x1, Pallas kernels, shards(): pl.pallas_call(functools.partial(kernel, owners, slots, size), out_shape=...  29.6 us
    unnamed x1, local copies, waits for them, and re-layouts  0.72 us

profile of v7, /device:TPU:0, one launch (start us, length us, event | category | flops | bytes accessed | tf_op | source)
XLA Modules:
  0.0 30.3 jit_solution(14178343339065518398)
XLA Ops:
  0.0 29.6 %shard_map.37 = bf16[48,3072]{1,0:T(8,128)(2,1)S(1)} custom-call(bf16[48,24,128]{2,1,0:T(8,128)(2,1)} %q_hbm.1, bf16[48,24,128]{2,1,0:T(8,128)(2,1)} %k_hbm.1, bf16[48,24,128]{2,1,0:T(8,128)(2,1)} %v_hbm.1), custom_call_target="tpu_custom_call" | custom-call | tf_op jit(solution)/shard_map/pallas_call | solution.py:303
  29.6 0.7 %copy.5 = bf16[48,3072]{1,0:T(8,128)(2,1)} copy(bf16[48,3072]{1,0:T(8,128)(2,1)S(1)} %shard_map.37) | data formatting | bytes 589824

commit v8 on v5

--- a/solution.py
+++ b/solution.py
@@ -223,9 +223,10 @@
             if j == 0:
                 pl.when(high)(ask_across)
             if j == 1:
-                pl.when(high)(functools.partial(deliver, 0, opposite))
+                pl.when(high)(functools.partial(deliver, 0, opposite, range(half - 1)))
             if j == last:
                 pl.when(low)(functools.partial(deliver, last - 1, tail))
+                pl.when(high)(functools.partial(deliver, 0, opposite, range(half - 1, half)))
                 pl.when(high)(functools.partial(deliver, last - 1, opposite, front))
             attend(j, second)
             if j == last:

time: 30.4 us -> 30.5 us (level)
  no operation moved by 1% of the time
where the time goes in v8:
time: 30.5 us; the launch traced here: 30.3 us
  Pallas kernels  29.6 us (97%)
  local copies, waits for them, and re-layouts  0.72 us (2%)
    pallas_call x1, Pallas kernels, shards(): pl.pallas_call(functools.partial(kernel, owners, slots, size), out_shape=...  29.6 us
    unnamed x1, local copies, waits for them, and re-layouts  0.72 us

profile of v8, /device:TPU:0, one launch (start us, length us, event | category | flops | bytes accessed | tf_op | source)
XLA Modules:
  0.0 30.3 jit_solution(6278045682466487344)
XLA Ops:
  0.0 29.6 %shard_map.37 = bf16[48,3072]{1,0:T(8,128)(2,1)S(1)} custom-call(bf16[48,24,128]{2,1,0:T(8,128)(2,1)} %q_hbm.1, bf16[48,24,128]{2,1,0:T(8,128)(2,1)} %k_hbm.1, bf16[48,24,128]{2,1,0:T(8,128)(2,1)} %v_hbm.1), custom_call_target="tpu_custom_call" | custom-call | tf_op jit(solution)/shard_map/pallas_call | solution.py:269
  29.6 0.7 %copy.5 = bf16[48,3072]{1,0:T(8,128)(2,1)} copy(bf16[48,3072]{1,0:T(8,128)(2,1)S(1)} %shard_map.37) | data formatting | bytes 589824
